TPU v7x, 256 devices: a whole 4x4x8 slice. The times are simulated.
256 devices in a mesh: branch: 32 (over y, z), tensor: 8 (over x, core).
Axes of the slice: x: 4, y: 4, z: 8, core: 2. Of those that a mesh axis runs over, the one named last changes fastest.
Arguments:
- layer_input: bfloat16 [16384, 5120], P(('branch', 'tensor')), may hold values from -360 to 360
- norm_gain: float32 [5120], replicated, may hold values from 0.25 to 1.75
- projection_weight: bfloat16 [5120, 5120], P(None, 'tensor'), may hold values from -0.078125 to 0.078125
- output_weight: bfloat16 [3072, 5120], P('tensor'), may hold values from -3 to 3
- prompt_cache: bfloat16 [2048, 2048], P(None, 'tensor'), may hold values from -1800 to 1800
- subtree_cache: bfloat16 [2, 16384, 2048], P(None, 'branch', 'tensor'), may hold values from -6 to 6
- parents: int32 [2, 32], replicated, may hold values from 0 to 31
- leaf_scores: float32 [32], P('branch'), may hold values from 0.3 to 1
Outputs:
- attn_output: bfloat16 [16384, 5120], P(('branch', 'tensor'))
- subtree_min: float32 [2, 32], P(None, 'branch')
- subtree_product: float32 [2, 32], P(None, 'branch')
Inputs may be any that keep to these rules, and one draw needn't show every extreme that they name: parents[0, j] is the parent in level one of node j of level two; parents[1, j] is the parent in level two of new node j. Node j of every level is held by branch index j.
All inputs are finite; a program needn't handle non-finite values.
Results may differ from a plain program's by a relative error of at most 0.015.
Values may be sent and summed in bfloat16 or wider, within the bound.
No kernel may reach another device: no remote copies, remote signals or barrier semaphores. Data moves between devices by JAX's collectives and lax.ppermute only.
A program may use at most 128 MiB of HBM per device.

v0:
```python
import jax
import jax.numpy as jnp
from jax import lax
from jax.sharding import PartitionSpec as P

HEAD_SIZE = 128
SEGMENT_TOKENS = 512
PROMPT_TOKENS = 2048
THETA = 1000000.0
EPSILON = 1e-06


def from_everyone(x, axis):
    count = lax.axis_size(axis)
    return lax.all_to_all(jnp.broadcast_to(x[None], (count, *x.shape)), axis, 0, 0, tiled=True)


def all_in_one(x, axis):
    leaves = jax.tree.leaves(x)
    sequence = sorted(range(len(leaves)), key=lambda k: -leaves[k].size)
    width = (1, *leaves[sequence[0]].shape)[-1]
    lines = [
        jnp.pad(leaves[k].reshape(-1), (0, -leaves[k].size % width)).reshape(-1, width)
        for k in sequence
    ]
    both, at, found = (from_everyone(jnp.concatenate(lines), axis), 0, {})
    for k, line in zip(sequence, lines):
        piece = both[:, at : at + len(line)].reshape(len(both), -1)
        found[k] = piece[:, : leaves[k].size].reshape(-1, *leaves[k].shape)
        at += len(line)
    numbers = iter(range(len(leaves)))
    return jax.tree.map(lambda _: found[next(numbers)], x)


def combined_pairwise(pieces, combine):
    while len(jax.tree.leaves(pieces)[0]) > 1:
        pieces = jax.vmap(combine)(
            *(jax.tree.map(lambda part: part[side::2], pieces) for side in (0, 1))
        )
    return jax.tree.map(lambda part: part[0], pieces)


def combined_all(x, axis, combine):
    pieces = all_in_one(x, axis)
    return combined_pairwise(pieces, combine)


def normalize(inputs, gain):
    wide = inputs.astype(jnp.float32)
    scale = lax.rsqrt(jnp.mean(wide * wide, axis=-1, keepdims=True) + EPSILON)
    return (wide * scale * gain).astype(jnp.bfloat16)


def rotate(vectors, offset):
    half = vectors.shape[-1] // 2
    freq = THETA ** (-jnp.arange(half, dtype=jnp.float32) * 2.0 / vectors.shape[-1])
    places = (offset + jnp.arange(vectors.shape[0])).astype(jnp.float32)
    angle = places[:, None] * freq[None, :]
    shape = (vectors.shape[0],) + (1,) * (vectors.ndim - 2) + (half,)
    cosine = jnp.cos(angle).reshape(shape)
    sine = jnp.sin(angle).reshape(shape)
    front = vectors[..., :half]
    back = vectors[..., half:]
    return jnp.concatenate([front * cosine - back * sine, back * cosine + front * sine], -1)


def attend(queries, context):
    keys = context[:, :, 0, :]
    values = context[:, :, 1, :]
    scale = queries.shape[-1] ** (-0.5)
    scores = jnp.einsum("skgd,lkd->kgsl", queries, keys, preferred_element_type=jnp.float32) * scale
    total = context.shape[0]
    count = queries.shape[0]
    key_place = jnp.arange(total)
    query_place = jnp.arange(count) + total - count
    visible = key_place[None, :] <= query_place[:, None]
    scores = jnp.where(visible, scores, -jnp.inf)
    top = jnp.max(scores, axis=-1, keepdims=True)
    expos = jnp.exp(scores - top)
    weights = (expos / jnp.sum(expos, axis=-1, keepdims=True)).astype(jnp.bfloat16)
    mixed = jnp.einsum("kgsl,lkd->skgd", weights, values, preferred_element_type=jnp.float32)
    return mixed.astype(jnp.bfloat16).reshape(count, -1)


def pair_combine(left, right):
    return (jnp.minimum(left[0], right[0]), left[1] * right[1])


def per_device(
    layer_input,
    norm_gain,
    projection_weight,
    output_weight,
    prompt_cache,
    subtree_cache,
    parents,
    leaf_scores,
):
    kv_heads = prompt_cache.shape[1] // (2 * HEAD_SIZE)
    group = projection_weight.shape[1] // (kv_heads * HEAD_SIZE) - 2
    offset = PROMPT_TOKENS + 2 * SEGMENT_TOKENS
    normed = normalize(layer_input, norm_gain)
    packed = jnp.dot(
        lax.all_gather(normed, "tensor", axis=0, tiled=True),
        projection_weight,
        preferred_element_type=jnp.float32,
    )
    packed = packed.reshape(SEGMENT_TOKENS, kv_heads, group + 2, HEAD_SIZE)
    queries = rotate(packed[:, :, :group, :], offset).astype(jnp.bfloat16)
    keys = rotate(packed[:, :, group, :], offset).astype(jnp.bfloat16)
    values = packed[:, :, group + 1, :].astype(jnp.bfloat16)
    own = jnp.stack([keys, values], 2)
    second = parents[1]
    first = parents[0][second]
    position = lax.axis_index("branch")
    held = lax.all_to_all(subtree_cache[None], "branch", split_axis=2, concat_axis=0, tiled=True)
    tree_levels = jnp.arange(2, dtype=jnp.int32)
    picks = jnp.stack([first, second], 1)
    outgoing = held[picks, tree_levels[None, :]]
    arrived = lax.all_to_all(outgoing, "branch", split_axis=0, concat_axis=2, tiled=True)
    blocks = arrived[0]
    blocks = blocks.reshape(2 * SEGMENT_TOKENS, kv_heads, 2, HEAD_SIZE)
    prompt = prompt_cache.reshape(-1, kv_heads, 2, HEAD_SIZE)
    context = jnp.concatenate([prompt, blocks, own], 0)
    mixed = attend(queries, context)
    partial_term = jnp.dot(mixed, output_weight, preferred_element_type=jnp.float32)
    summed = lax.psum_scatter(
        partial_term.astype(jnp.bfloat16).astype(jnp.float32).astype(jnp.bfloat16),
        "tensor",
        scatter_dimension=0,
        tiled=True,
    )
    nodes = jnp.arange(parents.shape[1], dtype=jnp.int32)
    marks = jnp.stack([nodes == first[position], nodes == second[position]], 0)
    filled = jnp.where(marks, leaf_scores[0], 1.0)
    lowest, product = combined_all((filled, filled), "branch", pair_combine)
    subtree_min = lax.dynamic_slice_in_dim(lowest, position, 1, 1)
    subtree_product = lax.dynamic_slice_in_dim(product, position, 1, 1)
    return (summed, subtree_min, subtree_product)


def solution(mesh):
    placed = (
        P(("branch", "tensor"), None),
        P(),
        P(None, "tensor"),
        P("tensor", None),
        P(None, "tensor"),
        P(None, "branch", "tensor"),
        P(),
        P("branch"),
    )
    return jax.shard_map(
        per_device,
        mesh=mesh,
        in_specs=placed,
        out_specs=(P(("branch", "tensor"), None), P(None, "branch"), P(None, "branch")),
        check_vma=False,
    )
```

profile of v0, /device:TPU:8, one launch (start us, length us, event | category | flops | bytes accessed | tf_op | source)
XLA Modules:
  0.0 169.4 jit_solution(4992892851186095734)
XLA Ops:
  7.2 0.0 all-gather.2.cloned.1.call-start
  7.2 1.3 fusion.4
  8.5 2.2 %fusion.6 = bf16[64,5120]{1,0:T(8,128)(2,1)} fusion(bf16[64,5120]{1,0:T(8,128)(2,1)} %param.8, f32[5120]{0:T(1024)} %param.9, f32[64]{0:T(128)S(1)} %add_rsqrt_fusion), kind=kLoop, calls=%fused_computation.16 | loop fusion | flops 1310720 | bytes 1331456 | tf_op jit(solution)/shard_map/convert_element_type | solution.py:51
  10.7 2.4 %copy.95 = bf16[2,512,256]{2,0,1:T(2,128)(2,1)} copy(bf16[2,512,256]{2,1,0:T(8,128)(2,1)} %param.13) | data formatting | bytes 1048576 | tf_op args[5]
  13.1 11.7 %all-to-all-start = ((bf16[1,2,512,256]{3,1,0,2:T(2,128)(2,1)}), bf16[1,2,512,256]{3,1,0,2:T(2,128)(2,1)S(1)}, u32[]{:S(2)}, u32[]{:S(2)}) async-start(bf16[1,2,512,256]{3,1,0,2:T(2,128)(2,1)} %bitcast.82), calls=%async_computation | async-start | bytes 1048576 | tf_op jit(solution)/shard_map/all_to_all | solution.py:116
  24.8 0.7 fusion.30
  25.5 0.8 fusion.36
  26.3 0.7 gather_fusion
  27.0 0.1 copy.71
  27.1 0.1 reshape.412
  27.2 1.5 copy.67
  28.7 0.7 copy.76
  29.4 1.8 %multiply_cosine_fusion = (f32[512,64]{1,0:T(8,128)}, f32[512,64]{1,0:T(8,128)}) fusion(f32[64]{0:T(128)S(1)} %multiply_power_fusion, f32[512]{0:T(512)S(1)} %fusion.29), kind=kLoop, calls=%fused_computation.31 | loop fusion | flops 32768 | bytes 264448 | tf_op jit(solution)/shard_map/cos | solution.py:60
  31.2 9.0 %all-to-all-done = bf16[1,2,512,256]{3,1,0,2:T(2,128)(2,1)S(1)} async-done(((bf16[1,2,512,256]{3,1,0,2:T(2,128)(2,1)}), bf16[1,2,512,256]{3,1,0,2:T(2,128)(2,1)S(1)}, u32[]{:S(2)}, u32[]{:S(2)}) %all-to-all-start) | async-done | bytes 524320 | tf_op jit(solution)/shard_map/all_to_all | solution.py:116
  40.3 0.1 copy.94
  40.4 1.5 gather_fusion.1
  41.9 7.0 %all-to-all-start.1 = ((bf16[32,2,16,256]{3,2,1,0:T(8,128)(2,1)}), bf16[32,2,16,256]{3,2,1,0:T(8,128)(2,1)S(1)}, u32[]{:S(2)}, u32[]{:S(2)}) async-start(bf16[32,2,16,256]{3,2,1,0:T(8,128)(2,1)} %bitcast.10), calls=%async_computation.1 | async-start | bytes 1048576 | tf_op jit(solution)/shard_map/all_to_all | solution.py:120
  48.9 0.2 reduce-scatter.2.cloned.1.call-start
  49.1 1.5 iota_compare_fusion
  50.6 13.0 %all-to-all-done.1 = bf16[32,2,16,256]{3,2,1,0:T(8,128)(2,1)S(1)} async-done(((bf16[32,2,16,256]{3,2,1,0:T(8,128)(2,1)}), bf16[32,2,16,256]{3,2,1,0:T(8,128)(2,1)S(1)}, u32[]{:S(2)}, u32[]{:S(2)}) %all-to-all-start.1) | async-done | bytes 524320 | tf_op jit(solution)/shard_map/all_to_all | solution.py:120
  63.7 0.8 copy.72
  64.5 1.2 reshape_squeeze.3
  65.7 0.9 copy.77
  66.6 8.4 %fusion.37 = f32[512,640]{0,1:T(8,128)S(1)} fusion(bf16[512,5120]{1,0:T(8,128)(2,1)} %all-gather.2.cloned.1.call-done, bf16[5120,640]{1,0:T(8,128)(2,1)} %param.10), kind=kOutput, calls=%fused_computation.80 | convolution fusion | flops 3355443200 | bytes 13107200 | tf_op jit(solution)/shard_map/dot_general | solution.py:103
  75.0 0.9 fusion.34
  76.0 0.1 copy.89
  76.1 0.1 copy.88
  76.2 1.9 %fusion.25 = (bf16[512,1,1,64]{3,0,2,1:T(8,128)(2,1)}, bf16[512,1,1,64]{3,0,2,1:T(8,128)(2,1)}) fusion(f32[512,1,128]{2,0,1:T(8,128)S(1)} %bitcast.85, f32[64]{0:T(128)S(1)} %multiply_power_fusion, f32[512]{0:T(512)S(1)} %fusion.29), kind=kLoop, calls=%fused_computation.43 | loop fusion | flops 294912 | bytes 395520 | tf_op jit(solution)/shard_map/concatenate | solution.py:64
  78.1 2.2 %copy.91 = f32[512,1,3,64]{3,0,2,1:T(8,128)} copy(f32[512,1,3,64]{0,3,2,1:T(8,128)} %get-tuple-element.5) | data formatting | bytes 786432
  80.3 2.2 %copy.90 = f32[512,1,3,64]{3,0,2,1:T(8,128)} copy(f32[512,1,3,64]{0,3,2,1:T(8,128)} %get-tuple-element.6) | data formatting | bytes 786432
  82.5 2.6 %fusion.11 = (bf16[512,3,64]{2,0,1:T(8,128)(2,1)}, bf16[512,3,64]{2,0,1:T(8,128)(2,1)}) fusion(f32[512,1,3,64]{3,0,2,1:T(8,128)} %copy.91, f32[512,1,3,64]{3,0,2,1:T(8,128)} %copy.90, f32[512,64]{1,0:T(8,128)} %get-tuple-element.12, f32[512,64]{1,0:T(8,128)} %get-tuple-element.11), kind=kLoop, calls=%fused_computation.25 | loop fusion | flops 786432 | bytes 1441792 | tf_op jit(solution)/shard_map/concatenate | solution.py:64
  85.1 2.4 %maximum_maximum_fusion = bf16[3584,1,2,128]{3,0,2,1:T(8,128)(2,1)} fusion(bf16[512,1,1,128]{3,0,2,1:T(8,128)(2,1)S(1)} %copy.89, bf16[512,1,1,64]{3,0,2,1:T(8,128)(2,1)} %get-tuple-element.8, bf16[512,1,1,64]{3,0,2,1:T(8,128)(2,1)} %get-tuple-element.7, bf16[1024,1,2,128]{3,0,2,1:T(8,128)(2,1)S(1)} %copy-done.2, bf16[2048,1,2,128]{3,0,2,1:T(8,128)(2,1)S(1)} %copy.76), kind=kLoop, calls=%fused_computation.11 | loop fusion | flops 9175040 | bytes 3670016 | tf_op jit(solution)/shard_map/concatenate | solution.py:124
  87.5 5.6 %fusion.1 = (f32[3,512]{1,0:T(4,128)S(1)}, f32[3584,512,3]{1,0,2:T(8,128)S(1)}) fusion(pred[512,3584]{0,1:T(8,128)(4,1)S(1)} %iota_compare_fusion, bf16[512,3,64]{2,0,1:T(8,128)(2,1)} %get-tuple-element.4, bf16[512,3,64]{2,0,1:T(8,128)(2,1)} %get-tuple-element.3, bf16[3584,1,2,128]{3,0,2,1:T(8,128)(2,1)} %maximum_maximum_fusion), kind=kOutput, calls=%fused_computation.6 | convolution fusion | flops 1426586112 | bytes 25565184 | tf_op jit(solution)/shard_map/skgd,lkd->kgsl/dot_general | solution.py:71
  93.1 7.3 %copy-done = f32[3584,512,3]{1,0,2:T(8,128)} copy-done((f32[3584,512,3]{1,0,2:T(8,128)}, f32[3584,512,3]{1,0,2:T(8,128)S(1)}, u32[]{:S(2)}) %copy-start) | copy-done | bytes 22020120
  100.4 5.0 %fusion = f32[3,512]{1,0:T(4,128)S(1)} fusion(f32[3584,512,3]{1,0,2:T(8,128)S(1)} %get-tuple-element.17, f32[3,512]{1,0:T(4,128)S(1)} %get-tuple-element.16, pred[512,3584]{0,1:T(8,128)(4,1)S(1)} %iota_compare_fusion), kind=kLoop, calls=%fused_computation.5 | loop fusion | flops 22018560 | bytes 23867392 | tf_op jit(solution)/shard_map/reduce_sum | solution.py:80
  105.5 11.2 %fusion.7 = bf16[128,3,512]{2,0,1:T(8,128)(2,1)S(1)} fusion(f32[3,512]{1,0:T(4,128)S(1)} %fusion, f32[3,512]{1,0:T(4,128)S(1)} %get-tuple-element.16, f32[3584,512,3]{1,0,2:T(8,128)} %copy-done, pred[512,3584]{0,1:T(8,128)(4,1)S(1)} %iota_compare_fusion, bf16[3584,1,2,128]{3,0,2,1:T(8,128)(2,1)} %maximum_maximum_fusion), kind=kOutput, calls=%fused_computation.17 | convolution fusion | flops 1437007872 | bytes 25178112 | tf_op jit(solution)/shard_map/kgsl,lkd->skgd/dot_general | solution.py:81
  116.7 4.7 %convolution_convert_fusion = bf16[512,5120]{1,0:T(8,128)(2,1)} fusion(bf16[512,384]{0,1:T(8,128)(2,1)S(1)} %bitcast.92, bf16[384,5120]{1,0:T(8,128)(2,1)S(1)} %copy-done.1), kind=kOutput, calls=%fused_computation.9 | convolution fusion | flops 2015887360 | bytes 9568256 | tf_op jit(solution)/shard_map/dot_general | solution.py:126
  122.1 0.6 dynamic_slice.16
  122.7 0.6 constant_dynamic-slice_fusion
  123.2 0.7 iota_compare_fusion.1
  123.9 0.7 iota_compare_fusion.2
  124.6 0.1 reshape.422
  124.7 15.4 %all_to_all.38 = f32[32,1,128]{2,1,0:T(1,128)S(1)} all-to-all(f32[32,1,128]{2,1,0:T(1,128)S(1)} %reshape.422), channel_id=1, replica_groups=mesh['branch'=32,'tensor'=8] {'branch'}, dimensions={0} | all-to-all | bytes 32768 | tf_op jit(solution)/shard_map/all_to_all | solution.py:15
  140.2 0.5 broadcast.216
  140.7 0.7 reduce.6
  141.4 0.1 reshape.423
  141.6 0.7 dynamic-slice_reduce_fusion
  142.4 20.1 %reduce-scatter.2.cloned.1.call-done = bf16[64,5120]{1,0:T(8,128)(2,1)} async-done(((bf16[512,5120]{1,0:T(8,128)(2,1)}), bf16[64,5120]{1,0:T(8,128)(2,1)}) %reduce-scatter.2.cloned.1.call-update) | async-done | bytes 655376 | tf_op jit(solution)/shard_map/reduce_scatter | solution.py:127
  (30 shorter events, 0.2 us)
Async XLA Ops:
  7.2 59.4 %all-gather.2.cloned.1.call-start = ((), (), s32[]{:S(2)}) async-start(), calls=%async_computation.4 | async-start | bytes 5898240 | tf_op jit(solution)/shard_map/all_gather | solution.py:104
  13.1 27.2 %all-to-all-start = ((bf16[1,2,512,256]{3,1,0,2:T(2,128)(2,1)}), bf16[1,2,512,256]{3,1,0,2:T(2,128)(2,1)S(1)}, u32[]{:S(2)}, u32[]{:S(2)}) async-start(bf16[1,2,512,256]{3,1,0,2:T(2,128)(2,1)} %bitcast.82), calls=%async_computation | async-start | bytes 1048576 | tf_op jit(solution)/shard_map/all_to_all | solution.py:116
  41.9 21.8 %all-to-all-start.1 = ((bf16[32,2,16,256]{3,2,1,0:T(8,128)(2,1)}), bf16[32,2,16,256]{3,2,1,0:T(8,128)(2,1)S(1)}, u32[]{:S(2)}, u32[]{:S(2)}) async-start(bf16[32,2,16,256]{3,2,1,0:T(8,128)(2,1)} %bitcast.10), calls=%async_computation.1 | async-start | bytes 1048576 | tf_op jit(solution)/shard_map/all_to_all | solution.py:120
  48.9 113.6 %reduce-scatter.2.cloned.1.call-start = ((), (), s32[]{:S(2)}) async-start(), calls=%async_computation.5 | async-start | bytes 5898240 | tf_op jit(solution)/shard_map/reduce_scatter | solution.py:127
  78.1 7.0 %copy-start.2 = (bf16[1024,1,2,128]{3,0,2,1:T(8,128)(2,1)S(1)}, bf16[1024,1,2,128]{3,0,2,1:T(8,128)(2,1)}, u32[]{:S(2)}) copy-start(bf16[1024,1,2,128]{3,0,2,1:T(8,128)(2,1)} %copy.77) | copy-start | bytes 1572868
  93.1 7.3 %copy-start = (f32[3584,512,3]{1,0,2:T(8,128)}, f32[3584,512,3]{1,0,2:T(8,128)S(1)}, u32[]{:S(2)}) copy-start(f32[3584,512,3]{1,0,2:T(8,128)S(1)} %get-tuple-element.17) | copy-start | bytes 66060292
  105.4 11.2 %copy-start.1 = (bf16[384,5120]{1,0:T(8,128)(2,1)S(1)}, bf16[384,5120]{1,0:T(8,128)(2,1)}, u32[]{:S(2)}) copy-start(bf16[384,5120]{1,0:T(8,128)(2,1)} %param.11) | copy-start | bytes 11796484
Sparse Core Ops, SparseCore 0:
  10.8 41.8 all-gather.1
  121.5 40.9 reduce-scatter.1
where the time goes:
time: 170 us; the launch traced here: 169 us
  waiting for transfers between devices  42.3 us (25%)
  matrix products  30 us (18%)
  local copies, waits for them, and re-layouts  26.2 us (15%)
  other arithmetic  21.5 us (13%)
  starting transfers between devices  19 us (11%)
  blocking collectives  15.4 us (9%)
  between operations  15 us (9%)
    reduce_scatter x1, waiting for transfers between devices, per_device(): lax.psum_scatter(partial_term.astype(jnp.bfloat16).astype(jnp.float32).as...  20.1 us
    unnamed x14, local copies, waits for them, and re-layouts  16.1 us
    all_to_all x1, blocking collectives, from_everyone(): lax.all_to_all(jnp.broadcast_to(x[None], (count, *x.shape)), axis, 0, 0,...  15.4 us
    all_to_all x1, waiting for transfers between devices, per_device(): lax.all_to_all(outgoing, 'branch', split_axis=0, concat_axis=2, tiled=True)  13 us
    all_to_all x1, starting transfers between devices, per_device(): lax.all_to_all(subtree_cache[None], 'branch', split_axis=2, concat_axis=0...  11.7 us
    dot_general x1, matrix products, attend(): jnp.einsum('kgsl,lkd->skgd', weights, values, preferred_element_type=jnp....  11.2 us
    all_to_all x1, waiting for transfers between devices, per_device(): lax.all_to_all(subtree_cache[None], 'branch', split_axis=2, concat_axis=0...  9.03 us
    dot_general x1, matrix products, per_device(): jnp.dot(lax.all_gather(normed, 'tensor', axis=0, tiled=True), projection_...  8.41 us
  transfers between devices with their start and end apart: 4, of which 3 were waited for; matrix products, arithmetic and copies ran while one was open for 11% of the time, Pallas kernels for 0%

commit v1 on v0

--- a/solution.py
+++ b/solution.py
@@ -113,7 +113,10 @@
     second = parents[1]
     first = parents[0][second]
     position = lax.axis_index("branch")
-    held = lax.all_to_all(subtree_cache[None], "branch", split_axis=2, concat_axis=0, tiled=True)
+    part_2 = subtree_cache[None]
+    cells = jnp.split(part_2, lax.axis_size("branch"), axis=2)
+    arrived_2 = lax.all_to_all(jnp.stack(cells), "branch", 0, 0)
+    held = jnp.concatenate(arrived_2, axis=0)
     tree_levels = jnp.arange(2, dtype=jnp.int32)
     picks = jnp.stack([first, second], 1)
     outgoing = held[picks, tree_levels[None, :]]

time: 170 us -> 212 us (1.25); the launches traced: 169 us -> 209 us
  local copies, waits for them, and re-layouts: 26.2 us -> 65.9 us
    unnamed x14 -> x44, local copies, waits for them, and re-layouts: 16.1 us -> 54.5 us
  transfers between devices with their start and end apart: 4 -> 4, of which waited for: 3 -> 3; matrix products, arithmetic and copies ran while one was open for 11% -> 28% of each run, Pallas kernels for 0% -> 0%
where the time goes in v1:
time: 212 us; the launch traced here: 209 us
  local copies, waits for them, and re-layouts  65.9 us (31%)
  waiting for transfers between devices  42.3 us (20%)
  matrix products  30 us (14%)
  other arithmetic  21.5 us (10%)
  starting transfers between devices  19 us (9%)
  blocking collectives  15.4 us (7%)
  between operations  15 us (7%)
    unnamed x44, local copies, waits for them, and re-layouts  54.5 us
    reduce_scatter x1, waiting for transfers between devices, per_device(): lax.psum_scatter(partial_term.astype(jnp.bfloat16).astype(jnp.float32).as...  20.2 us
    all_to_all x1, blocking collectives, from_everyone(): lax.all_to_all(jnp.broadcast_to(x[None], (count, *x.shape)), axis, 0, 0,...  15.4 us
    all_to_all x1, waiting for transfers between devices, per_device(): lax.all_to_all(outgoing, 'branch', split_axis=0, concat_axis=2, tiled=True)  13.1 us
    all_to_all x1, starting transfers between devices, per_device(): arrived_2 = lax.all_to_all(jnp.stack(cells), 'branch', 0, 0)  11.8 us
    dot_general x1, matrix products, attend(): jnp.einsum('kgsl,lkd->skgd', weights, values, preferred_element_type=jnp....  11.2 us
    all_to_all x1, waiting for transfers between devices, per_device(): arrived_2 = lax.all_to_all(jnp.stack(cells), 'branch', 0, 0)  9.07 us
    dot_general x1, matrix products, per_device(): jnp.dot(lax.all_gather(normed, 'tensor', axis=0, tiled=True), projection_...  8.41 us
  transfers between devices with their start and end apart: 4, of which 3 were waited for; matrix products, arithmetic and copies ran while one was open for 28% of the time, Pallas kernels for 0%

profile of v1, /device:TPU:8, one launch (start us, length us, event | category | flops | bytes accessed | tf_op | source)
XLA Modules:
  0.0 209.1 jit_solution(2922210674990851406)
XLA Ops:
  7.2 1.3 fusion.4
  8.5 2.2 %fusion.6 = bf16[64,5120]{1,0:T(8,128)(2,1)} fusion(bf16[64,5120]{1,0:T(8,128)(2,1)} %param.8, f32[5120]{0:T(1024)} %param.9, f32[64]{0:T(128)S(1)} %add_rsqrt_fusion), kind=kLoop, calls=%fused_computation.16 | loop fusion | flops 1310720 | bytes 1331456 | tf_op jit(solution)/shard_map/convert_element_type | solution.py:51
  10.7 1.3 constant_dynamic-update-slice_fusion.31
  12.0 1.3 constant_dynamic-update-slice_fusion.30
  13.4 1.3 constant_dynamic-update-slice_fusion.29
  14.7 1.3 constant_dynamic-update-slice_fusion.28
  17.3 1.3 constant_dynamic-update-slice_fusion.26
  18.6 1.3 constant_dynamic-update-slice_fusion.25
  20.0 1.3 constant_dynamic-update-slice_fusion.24
  23.9 1.3 constant_dynamic-update-slice_fusion.21
  25.2 1.3 constant_dynamic-update-slice_fusion.20
  26.5 1.3 constant_dynamic-update-slice_fusion.19
  27.8 1.3 constant_dynamic-update-slice_fusion.18
  31.8 1.3 constant_dynamic-update-slice_fusion.15
  33.1 1.3 constant_dynamic-update-slice_fusion.14
  34.4 1.3 constant_dynamic-update-slice_fusion.13
  35.8 1.3 constant_dynamic-update-slice_fusion.12
  37.1 1.3 constant_dynamic-update-slice_fusion.11
  38.4 1.3 constant_dynamic-update-slice_fusion.10
  39.7 1.3 constant_dynamic-update-slice_fusion.9
  41.0 1.3 constant_dynamic-update-slice_fusion.8
  43.7 1.3 constant_dynamic-update-slice_fusion.6
  45.0 1.3 constant_dynamic-update-slice_fusion.5
  47.6 1.3 constant_dynamic-update-slice_fusion.3
  48.9 1.3 constant_dynamic-update-slice_fusion.2
  50.3 1.3 constant_dynamic-update-slice_fusion.1
  51.6 1.3 constant_dynamic-update-slice_fusion
  52.9 11.8 %all-to-all-start = ((bf16[32,1,2,16,256]{4,3,2,1,0:T(8,128)(2,1)}), bf16[32,1,2,16,256]{4,3,2,1,0:T(8,128)(2,1)S(1)}, u32[]{:S(2)}, u32[]{:S(2)}) async-start(bf16[32,1,2,16,256]{4,3,2,1,0:T(8,128)(2,1)} %constant_dynamic-update-slice_fusion), calls=%async_computation | async-start | bytes 1048576 | tf_op jit(solution)/shard_map/all_to_all | solution.py:118
  67.0 1.5 copy.42
  69.2 1.8 multiply_cosine_fusion
  71.1 9.1 %all-to-all-done = bf16[32,1,2,16,256]{4,3,2,1,0:T(8,128)(2,1)S(1)} async-done(((bf16[32,1,2,16,256]{4,3,2,1,0:T(8,128)(2,1)}), bf16[32,1,2,16,256]{4,3,2,1,0:T(8,128)(2,1)S(1)}, u32[]{:S(2)}, u32[]{:S(2)}) %all-to-all-start) | async-done | bytes 524320 | tf_op jit(solution)/shard_map/all_to_all | solution.py:118
  80.1 1.5 gather_fusion.1
  81.6 7.0 %all-to-all-start.1 = ((bf16[32,2,16,256]{3,2,1,0:T(8,128)(2,1)}), bf16[32,2,16,256]{3,2,1,0:T(8,128)(2,1)S(1)}, u32[]{:S(2)}, u32[]{:S(2)}) async-start(bf16[32,2,16,256]{3,2,1,0:T(8,128)(2,1)} %bitcast.40), calls=%async_computation.1 | async-start | bytes 1048576 | tf_op jit(solution)/shard_map/all_to_all | solution.py:123
  88.9 1.5 iota_compare_fusion
  90.4 13.1 %all-to-all-done.1 = bf16[32,2,16,256]{3,2,1,0:T(8,128)(2,1)S(1)} async-done(((bf16[32,2,16,256]{3,2,1,0:T(8,128)(2,1)}), bf16[32,2,16,256]{3,2,1,0:T(8,128)(2,1)S(1)}, u32[]{:S(2)}, u32[]{:S(2)}) %all-to-all-start.1) | async-done | bytes 524320 | tf_op jit(solution)/shard_map/all_to_all | solution.py:123
  106.3 8.4 %fusion.37 = f32[512,640]{0,1:T(8,128)S(1)} fusion(bf16[512,5120]{1,0:T(8,128)(2,1)} %all-gather.2.cloned.1.call-done, bf16[5120,640]{1,0:T(8,128)(2,1)} %param.10), kind=kOutput, calls=%fused_computation.142 | convolution fusion | flops 3355443200 | bytes 13107200 | tf_op jit(solution)/shard_map/dot_general | solution.py:103
  116.0 1.9 fusion.25
  117.8 2.2 %copy.61 = f32[512,1,3,64]{3,0,2,1:T(8,128)} copy(f32[512,1,3,64]{0,3,2,1:T(8,128)} %get-tuple-element.5) | data formatting | bytes 786432
  120.0 2.2 %copy.60 = f32[512,1,3,64]{3,0,2,1:T(8,128)} copy(f32[512,1,3,64]{0,3,2,1:T(8,128)} %get-tuple-element.6) | data formatting | bytes 786432
  122.2 2.6 %fusion.11 = (bf16[512,3,64]{2,0,1:T(8,128)(2,1)}, bf16[512,3,64]{2,0,1:T(8,128)(2,1)}) fusion(f32[512,1,3,64]{3,0,2,1:T(8,128)} %copy.61, f32[512,1,3,64]{3,0,2,1:T(8,128)} %copy.60, f32[512,64]{1,0:T(8,128)} %get-tuple-element.12, f32[512,64]{1,0:T(8,128)} %get-tuple-element.11), kind=kLoop, calls=%fused_computation.23 | loop fusion | flops 786432 | bytes 1441792 | tf_op jit(solution)/shard_map/concatenate | solution.py:64
  124.8 2.4 %maximum_maximum_fusion = bf16[3584,1,2,128]{3,0,2,1:T(8,128)(2,1)} fusion(bf16[512,1,1,128]{3,0,2,1:T(8,128)(2,1)S(1)} %copy.59, bf16[512,1,1,64]{3,0,2,1:T(8,128)(2,1)} %get-tuple-element.8, bf16[512,1,1,64]{3,0,2,1:T(8,128)(2,1)} %get-tuple-element.7, bf16[1024,1,2,128]{3,0,2,1:T(8,128)(2,1)S(1)} %copy-done.2, bf16[2048,1,2,128]{3,0,2,1:T(8,128)(2,1)S(1)} %copy.48), kind=kLoop, calls=%fused_computation.11 | loop fusion | flops 9175040 | bytes 3670016 | tf_op jit(solution)/shard_map/concatenate | solution.py:127
  127.2 5.6 %fusion.1 = (f32[3,512]{1,0:T(4,128)S(1)}, f32[3584,512,3]{1,0,2:T(8,128)S(1)}) fusion(pred[512,3584]{0,1:T(8,128)(4,1)S(1)} %iota_compare_fusion, bf16[512,3,64]{2,0,1:T(8,128)(2,1)} %get-tuple-element.4, bf16[512,3,64]{2,0,1:T(8,128)(2,1)} %get-tuple-element.3, bf16[3584,1,2,128]{3,0,2,1:T(8,128)(2,1)} %maximum_maximum_fusion), kind=kOutput, calls=%fused_computation.6 | convolution fusion | flops 1426586112 | bytes 25565184 | tf_op jit(solution)/shard_map/skgd,lkd->kgsl/dot_general | solution.py:71
  132.9 7.3 %copy-done = f32[3584,512,3]{1,0,2:T(8,128)} copy-done((f32[3584,512,3]{1,0,2:T(8,128)}, f32[3584,512,3]{1,0,2:T(8,128)S(1)}, u32[]{:S(2)}) %copy-start) | copy-done | bytes 22020120
  140.2 5.0 %fusion = f32[3,512]{1,0:T(4,128)S(1)} fusion(f32[3584,512,3]{1,0,2:T(8,128)S(1)} %get-tuple-element.17, f32[3,512]{1,0:T(4,128)S(1)} %get-tuple-element.16, pred[512,3584]{0,1:T(8,128)(4,1)S(1)} %iota_compare_fusion), kind=kLoop, calls=%fused_computation.5 | loop fusion | flops 22018560 | bytes 23867392 | tf_op jit(solution)/shard_map/reduce_sum | solution.py:80
  145.2 11.2 %fusion.7 = bf16[128,3,512]{2,0,1:T(8,128)(2,1)S(1)} fusion(f32[3,512]{1,0:T(4,128)S(1)} %fusion, f32[3,512]{1,0:T(4,128)S(1)} %get-tuple-element.16, f32[3584,512,3]{1,0,2:T(8,128)} %copy-done, pred[512,3584]{0,1:T(8,128)(4,1)S(1)} %iota_compare_fusion, bf16[3584,1,2,128]{3,0,2,1:T(8,128)(2,1)} %maximum_maximum_fusion), kind=kOutput, calls=%fused_computation.17 | convolution fusion | flops 1437007872 | bytes 25178112 | tf_op jit(solution)/shard_map/kgsl,lkd->skgd/dot_general | solution.py:81
  156.4 4.7 %convolution_convert_fusion = bf16[512,5120]{1,0:T(8,128)(2,1)} fusion(bf16[512,384]{0,1:T(8,128)(2,1)S(1)} %bitcast.244, bf16[384,5120]{1,0:T(8,128)(2,1)S(1)} %copy-done.1), kind=kOutput, calls=%fused_computation.9 | convolution fusion | flops 2015887360 | bytes 9568256 | tf_op jit(solution)/shard_map/dot_general | solution.py:129
  164.5 15.4 %all_to_all.25 = f32[32,1,128]{2,1,0:T(1,128)S(1)} all-to-all(f32[32,1,128]{2,1,0:T(1,128)S(1)} %reshape.426), channel_id=1, replica_groups=mesh['branch'=32,'tensor'=8] {'branch'}, dimensions={0} | all-to-all | bytes 32768 | tf_op jit(solution)/shard_map/all_to_all | solution.py:15
  182.1 20.2 %reduce-scatter.2.cloned.1.call-done = bf16[64,5120]{1,0:T(8,128)(2,1)} async-done(((bf16[512,5120]{1,0:T(8,128)(2,1)}), bf16[64,5120]{1,0:T(8,128)(2,1)}) %reduce-scatter.2.cloned.1.call-update) | async-done | bytes 655376 | tf_op jit(solution)/shard_map/reduce_scatter | solution.py:130
  (60 shorter events, 21.3 us)
Async XLA Ops:
  7.2 99.1 %all-gather.2.cloned.1.call-start = ((), (), s32[]{:S(2)}) async-start(), calls=%async_computation.4 | async-start | bytes 5898240 | tf_op jit(solution)/shard_map/all_gather | solution.py:104
  52.9 27.2 %all-to-all-start = ((bf16[32,1,2,16,256]{4,3,2,1,0:T(8,128)(2,1)}), bf16[32,1,2,16,256]{4,3,2,1,0:T(8,128)(2,1)S(1)}, u32[]{:S(2)}, u32[]{:S(2)}) async-start(bf16[32,1,2,16,256]{4,3,2,1,0:T(8,128)(2,1)} %constant_dynamic-update-slice_fusion), calls=%async_computation | async-start | bytes 1048576 | tf_op jit(solution)/shard_map/all_to_all | solution.py:118
  81.6 21.8 %all-to-all-start.1 = ((bf16[32,2,16,256]{3,2,1,0:T(8,128)(2,1)}), bf16[32,2,16,256]{3,2,1,0:T(8,128)(2,1)S(1)}, u32[]{:S(2)}, u32[]{:S(2)}) async-start(bf16[32,2,16,256]{3,2,1,0:T(8,128)(2,1)} %bitcast.40), calls=%async_computation.1 | async-start | bytes 1048576 | tf_op jit(solution)/shard_map/all_to_all | solution.py:123
  88.6 113.7 %reduce-scatter.2.cloned.1.call-start = ((), (), s32[]{:S(2)}) async-start(), calls=%async_computation.5 | async-start | bytes 5898240 | tf_op jit(solution)/shard_map/reduce_scatter | solution.py:130
  117.8 7.0 %copy-start.2 = (bf16[1024,1,2,128]{3,0,2,1:T(8,128)(2,1)S(1)}, bf16[1024,1,2,128]{3,0,2,1:T(8,128)(2,1)}, u32[]{:S(2)}) copy-start(bf16[1024,1,2,128]{3,0,2,1:T(8,128)(2,1)} %copy.49) | copy-start | bytes 1572868
  132.8 7.3 %copy-start = (f32[3584,512,3]{1,0,2:T(8,128)}, f32[3584,512,3]{1,0,2:T(8,128)S(1)}, u32[]{:S(2)}) copy-start(f32[3584,512,3]{1,0,2:T(8,128)S(1)} %get-tuple-element.17) | copy-start | bytes 66060292
  145.2 11.2 %copy-start.1 = (bf16[384,5120]{1,0:T(8,128)(2,1)S(1)}, bf16[384,5120]{1,0:T(8,128)(2,1)}, u32[]{:S(2)}) copy-start(bf16[384,5120]{1,0:T(8,128)(2,1)} %param.11) | copy-start | bytes 11796484
Sparse Core Ops, SparseCore 0:
  10.8 41.8 all-gather.1
  161.3 40.9 reduce-scatter.1
